TPU v7x, 32 devices: a whole 2x2x4 slice. The times are simulated.
32 devices in a mesh: shard: 8 (over z, y), model: 4 (over x, core).
Axes of the slice: x: 2, y: 2, z: 4, core: 2. Of those that a mesh axis runs over, the one named last changes fastest.
Arguments:
- gradients: float32 [32, 128, 4096], P(None, 'shard', 'model'), may hold values from -6 to 6
- momentum: float32 [32, 128, 4096], P(None, 'shard', 'model'), may hold values from -6 to 6
- weights: float32 [32, 128, 4096], P(None, 'shard', 'model'), may hold values from -0.1875 to 0.1875
Outputs:
- new_weights: float32 [32, 128, 4096], P(None, 'shard', 'model')
- new_momentum: float32 [32, 128, 4096], P(None, 'shard', 'model')
All inputs are finite; a program needn't handle non-finite values.
Results may differ from a plain program's by a relative error of at most 0.00015.
Values sent between devices are 32-bit elements; how exact they have to be, the bound alone decides.
No kernel may reach another device: no remote copies, remote signals or barrier semaphores. Data moves between devices by JAX's collectives and lax.ppermute only.
A program may use at most 128 MiB of HBM per device.

v0:
```python
import jax
import jax.numpy as jnp
from jax import lax
from jax.sharding import PartitionSpec as P

ITERS = 4
hold_rate = 0.8
learn_rate = 1.0
HIGH = lax.Precision.HIGHEST


def mul(a, b):
    return jnp.einsum("mij,mjk->mik", a, b, precision=HIGH)


def direction(gram):
    eye = jnp.eye(gram.shape[-1], dtype=gram.dtype)
    squares = jnp.sum(gram * eye, axis=(1, 2), keepdims=True)
    scale = lax.rsqrt(squares + 1e-06)
    a = gram * scale * scale
    total = None
    for step in range(ITERS):
        q = 3.4445 * eye - 4.775 * a + 2.0315 * mul(a, a)
        total = q if total is None else mul(q, total)
        if step < ITERS - 1:
            a = mul(mul(q, a), q)
    return total * scale


def make(mesh):
    models = mesh.shape["model"]

    def on_device(gradients, momentum, weights):
        new_momentum = hold_rate * momentum + gradients
        whole = lax.all_to_all(new_momentum, "shard", split_axis=0, concat_axis=1, tiled=True)
        gram = jnp.einsum("mik,mjk->mij", whole, whole, precision=HIGH)
        mine = gram.shape[0] // models
        parts = lax.all_to_all(gram, "model", split_axis=0, concat_axis=0, tiled=True)
        gram = jnp.sum(parts.reshape(models, mine, *gram.shape[1:]), axis=0)
        turn = lax.all_gather(direction(gram), "model", axis=0, tiled=True)
        moved = mul(turn, whole)
        back = lax.all_to_all(moved, "shard", split_axis=1, concat_axis=0, tiled=True)
        new_weights = weights - learn_rate * back
        return (new_weights, new_momentum)

    return on_device


def solution(mesh):
    placed = P(None, "shard", "model")
    return jax.shard_map(
        make(mesh),
        mesh=mesh,
        in_specs=(placed, placed, placed),
        out_specs=(placed, placed),
        check_vma=False,
    )
```

profile of v0, /device:TPU:0, one launch (start us, length us, event | category | flops | bytes accessed | tf_op | source)
XLA Modules:
  0.0 138.1 jit_solution(6963360470699167812)
XLA Ops:
  0.6 2.7 %multiply_add_fusion = f32[32,16,1024]{2,1,0:T(8,128)S(1)} fusion(f32[32,16,1024]{2,1,0:T(8,128)} %param.3, f32[32,16,1024]{2,1,0:T(8,128)} %param.4), kind=kLoop, calls=%fused_computation.1 | loop fusion | flops 1048576 | bytes 6291456 | tf_op jit(solution)/shard_map/add | solution.py:34
  3.3 0.0 copy-start
  3.3 55.3 %all_to_all.41 = f32[32,16,1024]{2,1,0:T(8,128)S(1)} all-to-all(f32[32,16,1024]{2,1,0:T(8,128)S(1)} %multiply_add_fusion), channel_id=1, replica_groups=mesh['shard'=8,'model'=4] {'shard'}, dimensions={0} | all-to-all | bytes 4194304 | tf_op jit(solution)/shard_map/all_to_all | solution.py:35
  58.6 0.0 copy-done
  58.6 0.2 copy.7
  58.9 2.1 %fusion.7 = f32[4,128,128]{2,1,0:T(8,128)S(1)} fusion(f32[4,128,1024]{2,1,0:T(8,128)S(1)} %bitcast.37), kind=kOutput, calls=%fused_computation.21 | convolution fusion | flops 805306368 | bytes 2359296 | tf_op jit(solution)/shard_map/mik,mjk->mij/dot_general | solution.py:36
  60.9 8.6 %all_to_all.42 = f32[4,128,128]{2,1,0:T(8,128)S(1)} all-to-all(f32[4,128,128]{2,1,0:T(8,128)S(1)} %fusion.7), channel_id=1, replica_groups=mesh['shard'=8,'model'=4] {'model'}, dimensions={0} | all-to-all | bytes 524288 | tf_op jit(solution)/shard_map/all_to_all | solution.py:38
  69.5 0.6 select_reduce_fusion
  70.8 0.2 fusion.3
  71.1 0.2 fusion.4
  71.3 0.2 fusion.8
  71.5 0.2 fusion.2
  71.7 0.2 fusion.13
  71.9 0.2 fusion.9
  72.1 0.2 fusion.10
  72.3 0.2 fusion.1
  72.5 0.2 fusion.11
  72.8 0.2 fusion.14
  73.0 0.2 fusion.12
  73.2 0.2 fusion
  73.4 0.2 convolution_multiply_fusion
  73.6 5.8 %all-gather = f32[512,128]{1,0:T(8,128)S(1)} all-gather(f32[128,128]{1,0:T(8,128)S(1)} %convolution_multiply_fusion), channel_id=2, replica_groups=mesh['shard'=8,'model'=4] {'model'}, dimensions={0}, use_global_device_ids=true | all-gather | bytes 327680 | tf_op jit(solution)/shard_map/all_gather | solution.py:40
  79.4 1.9 %fusion.15 = f32[4,128,1024]{2,1,0:T(8,128)S(1)} fusion(f32[4,128,128]{2,1,0:T(8,128)S(1)} %bitcast.41, f32[4,128,1024]{2,1,0:T(8,128)S(1)} %bitcast.38), kind=kOutput, calls=%fused_computation.29 | convolution fusion | flops 805306368 | bytes 4456448 | tf_op jit(solution)/shard_map/mij,mjk->mik/dot_general | solution.py:13
  81.3 1.4 copy.8
  82.7 52.1 %all_to_all.43 = f32[4,128,1024]{2,0,1:T(4,128)S(1)} all-to-all(f32[4,128,1024]{2,0,1:T(4,128)S(1)} %copy.8), channel_id=1, replica_groups=mesh['shard'=8,'model'=4] {'shard'}, dimensions={1} | all-to-all | bytes 4194304 | tf_op jit(solution)/shard_map/all_to_all | solution.py:42
  134.8 0.0 copy-start.1
  134.8 1.2 copy.9
  136.0 0.4 copy-done.1
  136.3 1.7 %bitcast_subtract_fusion = f32[32,16,1024]{2,1,0:T(8,128)} fusion(f32[32,16,1024]{2,1,0:T(8,128)S(1)} %copy-done.1, f32[8,4,16,1024]{3,2,1,0:T(8,128)S(1)} %copy.9), kind=kLoop, calls=%fused_computation | loop fusion | flops 524288 | bytes 6291456 | tf_op jit(solution)/shard_map/sub | solution.py:43
  (1 shorter events, 0.0 us)
Async XLA Ops:
  3.3 55.4 %copy-start = (f32[32,16,1024]{2,1,0:T(8,128)}, f32[32,16,1024]{2,1,0:T(8,128)S(1)}, u32[]{:S(2)}) copy-start(f32[32,16,1024]{2,1,0:T(8,128)S(1)} %multiply_add_fusion) | copy-start | bytes 6291460
  134.8 1.6 %copy-start.1 = (f32[32,16,1024]{2,1,0:T(8,128)S(1)}, f32[32,16,1024]{2,1,0:T(8,128)}, u32[]{:S(2)}) copy-start(f32[32,16,1024]{2,1,0:T(8,128)} %param.5) | copy-start | bytes 6291460
where the time goes:
time: 138 us
  blocking collectives  122 us (88%)
  matrix products  6.62 us (5%)
  other arithmetic  5.03 us (4%)
  local copies, waits for them, and re-layouts  3.18 us (2%)
  between operations  1.48 us (1%)
    all_to_all x1, blocking collectives, on_device(): lax.all_to_all(new_momentum, 'shard', split_axis=0, concat_axis=1, tiled=...  55.3 us
    all_to_all x1, blocking collectives, on_device(): lax.all_to_all(moved, 'shard', split_axis=1, concat_axis=0, tiled=True)  52.1 us
    all_to_all x1, blocking collectives, on_device(): lax.all_to_all(gram, 'model', split_axis=0, concat_axis=0, tiled=True)  8.57 us
    all_gather x1, blocking collectives, on_device(): turn = lax.all_gather(direction(gram), 'model', axis=0, tiled=True)  5.78 us
    dot_general x14, matrix products, mul(): return jnp.einsum('mij,mjk->mik', a, b, precision=HIGH)  4.57 us

commit v1 on v0

--- a/solution.py
+++ b/solution.py
@@ -2,6 +2,7 @@
 import jax.numpy as jnp
 from jax import lax
 from jax.sharding import PartitionSpec as P
+from jax.lax import all_to_all, axis_size
 
 ITERS = 4
 hold_rate = 0.8
@@ -39,7 +40,11 @@
         gram = jnp.sum(parts.reshape(models, mine, *gram.shape[1:]), axis=0)
         turn = lax.all_gather(direction(gram), "model", axis=0, tiled=True)
         moved = mul(turn, whole)
-        back = lax.all_to_all(moved, "shard", split_axis=1, concat_axis=0, tiled=True)
+        pass_ratios = lambda array_in, along_axis: jnp.concatenate(
+            all_to_all(jnp.stack(jnp.split(array_in, axis_size(along_axis), 1)), along_axis, 0, 0),
+            0,
+        )
+        back = pass_ratios(moved, along_axis="shard")
         new_weights = weights - learn_rate * back
         return (new_weights, new_momentum)
 

time: 138 us -> 136 us (0.986)
  local copies, waits for them, and re-layouts: 3.18 us -> 0.41 us
where the time goes in v1:
time: 136 us
  blocking collectives  122 us (90%)
  matrix products  6.62 us (5%)
  other arithmetic  5.03 us (4%)
  between operations  1.54 us (1%)
    all_to_all x1, blocking collectives, on_device(): lax.all_to_all(new_momentum, 'shard', split_axis=0, concat_axis=1, tiled=...  55.3 us
    all_to_all x1, blocking collectives, on_device(): all_to_all(jnp.stack(jnp.split(array_in, axis_size(along_axis), 1)), alon...  52.2 us
    all_to_all x1, blocking collectives, on_device(): lax.all_to_all(gram, 'model', split_axis=0, concat_axis=0, tiled=True)  8.57 us
    all_gather x1, blocking collectives, on_device(): turn = lax.all_gather(direction(gram), 'model', axis=0, tiled=True)  5.78 us
    dot_general x14, matrix products, mul(): return jnp.einsum('mij,mjk->mik', a, b, precision=HIGH)  4.57 us

profile of v1, /device:TPU:0, one launch (start us, length us, event | category | flops | bytes accessed | tf_op | source)
XLA Modules:
  0.0 135.5 jit_solution(16316558857402077298)
XLA Ops:
  0.6 2.7 %multiply_add_fusion = f32[32,16,1024]{2,1,0:T(8,128)S(1)} fusion(f32[32,16,1024]{2,1,0:T(8,128)} %param.3, f32[32,16,1024]{2,1,0:T(8,128)} %param.4), kind=kLoop, calls=%fused_computation.1 | loop fusion | flops 1048576 | bytes 6291456 | tf_op jit(solution)/shard_map/add | solution.py:35
  3.3 0.0 copy-start
  3.3 55.3 %all_to_all.28 = f32[32,16,1024]{2,1,0:T(8,128)S(1)} all-to-all(f32[32,16,1024]{2,1,0:T(8,128)S(1)} %multiply_add_fusion), channel_id=1, replica_groups=mesh['shard'=8,'model'=4] {'shard'}, dimensions={0} | all-to-all | bytes 4194304 | tf_op jit(solution)/shard_map/all_to_all | solution.py:36
  58.6 0.0 copy-done
  58.6 0.2 copy.5
  58.9 2.1 %fusion.15 = f32[4,128,128]{2,1,0:T(8,128)S(1)} fusion(f32[4,128,1024]{2,1,0:T(8,128)S(1)} %bitcast.66), kind=kOutput, calls=%fused_computation.37 | convolution fusion | flops 805306368 | bytes 2359296 | tf_op jit(solution)/shard_map/mik,mjk->mij/dot_general | solution.py:37
  60.9 8.6 %all_to_all.29 = f32[4,128,128]{2,1,0:T(8,128)S(1)} all-to-all(f32[4,128,128]{2,1,0:T(8,128)S(1)} %fusion.15), channel_id=1, replica_groups=mesh['shard'=8,'model'=4] {'model'}, dimensions={0} | all-to-all | bytes 524288 | tf_op jit(solution)/shard_map/all_to_all | solution.py:39
  69.5 0.6 select_reduce_fusion
  70.8 0.2 fusion.3
  71.1 0.2 fusion.12
  71.3 0.2 fusion.16
  71.5 0.2 fusion.2
  71.7 0.2 fusion.21
  71.9 0.2 fusion.17
  72.1 0.2 fusion.18
  72.3 0.2 fusion.1
  72.5 0.2 fusion.19
  72.8 0.2 fusion.22
  73.0 0.2 fusion.20
  73.2 0.2 fusion
  73.4 0.2 convolution_multiply_fusion
  73.6 5.8 %all-gather = f32[512,128]{1,0:T(8,128)S(1)} all-gather(f32[128,128]{1,0:T(8,128)S(1)} %convolution_multiply_fusion), channel_id=2, replica_groups=mesh['shard'=8,'model'=4] {'model'}, dimensions={0}, use_global_device_ids=true | all-gather | bytes 327680 | tf_op jit(solution)/shard_map/all_gather | solution.py:41
  79.4 1.9 %fusion.23 = f32[4,128,1024]{2,1,0:T(8,128)S(1)} fusion(f32[4,128,128]{2,1,0:T(8,128)S(1)} %bitcast.69, f32[4,128,1024]{2,1,0:T(8,128)S(1)} %bitcast.67), kind=kOutput, calls=%fused_computation.45 | convolution fusion | flops 805306368 | bytes 4456448 | tf_op jit(solution)/shard_map/mij,mjk->mik/dot_general | solution.py:14
  81.5 0.0 copy-start.1
  81.5 52.2 %all_to_all.30 = f32[8,4,16,1024]{3,2,1,0:T(8,128)S(1)} all-to-all(f32[8,4,16,1024]{3,2,1,0:T(8,128)S(1)} %fusion.4), channel_id=1, replica_groups=mesh['shard'=8,'model'=4] {'shard'}, dimensions={0} | all-to-all | bytes 4194304 | tf_op jit(solution)/shard_map/all_to_all | solution.py:44
  133.8 0.0 copy-done.1
  133.8 1.7 %bitcast_subtract_fusion = f32[32,16,1024]{2,1,0:T(8,128)} fusion(f32[32,16,1024]{2,1,0:T(8,128)S(1)} %copy-done.1, f32[8,4,16,1024]{3,2,1,0:T(8,128)S(1)} %all_to_all.30), kind=kLoop, calls=%fused_computation | loop fusion | flops 524288 | bytes 6291456 | tf_op jit(solution)/shard_map/sub | solution.py:48
  (9 shorter events, 0.2 us)
Async XLA Ops:
  3.3 55.4 %copy-start = (f32[32,16,1024]{2,1,0:T(8,128)}, f32[32,16,1024]{2,1,0:T(8,128)S(1)}, u32[]{:S(2)}) copy-start(f32[32,16,1024]{2,1,0:T(8,128)S(1)} %multiply_add_fusion) | copy-start | bytes 6291460
  81.5 52.2 %copy-start.1 = (f32[32,16,1024]{2,1,0:T(8,128)S(1)}, f32[32,16,1024]{2,1,0:T(8,128)}, u32[]{:S(2)}) copy-start(f32[32,16,1024]{2,1,0:T(8,128)} %param.5) | copy-start | bytes 6291460
